TPU v7x, 32 devices: a whole 2x2x4 slice. The times are simulated.
32 devices in a mesh: rows: 8 (over z, x), cols: 4 (over y, core).
Axes of the slice: x: 2, y: 2, z: 4, core: 2. Of those that a mesh axis runs over, the one named last changes fastest.
Arguments:
- basis: float32 [8192, 4096], P('rows', 'cols'), may hold values from -119.66257 to 119.66257, as said below
- block: float32 [8192, 512], P('rows', 'cols'), may hold values from -1800 to 1800
Outputs:
- ortho: float32 [8192, 512], P('rows', 'cols')
- factors: float32 [4, 128, 128], P('cols')
Inputs may be any that keep to these rules, and one draw needn't show every extreme that they name: Under the inner product (sum over rows divided by 8192) the basis columns have squared norms between 0.6 and 1.9, and inner products of distinct basis columns are at most 0.05 in magnitude.
All inputs are finite; a program needn't handle non-finite values.
Results may differ from a plain program's by a relative error of at most 0.000076.
Values sent between devices are 32-bit elements; how exact they have to be, the bound alone decides.
No kernel may reach another device: no remote copies, remote signals or barrier semaphores. Data moves between devices by JAX's collectives and lax.ppermute only.
A program may use at most 64 MiB of HBM per device.

v0:
```python
import jax
import jax.numpy as jnp
from jax import lax
from jax.sharding import PartitionSpec as P

BLK = 128


def solve_block(lower_factor, vectors):
    return jax.scipy.linalg.solve_triangular(lower_factor, vectors, lower=True)


def body(basis, block):
    highest = lax.Precision.HIGHEST
    local_rows = basis.shape[0]
    inverse = 1.0 / (local_rows * lax.axis_size("rows"))
    width = block.shape[1]
    column_index = lax.axis_index("cols")

    def project(piece):
        return (
            lax.dot_general(
                basis,
                piece,
                (((0,), (0,)), ((), ())),
                precision=highest,
                preferred_element_type=jnp.float32,
            )
            * inverse
        )

    def expand(coef):
        return jnp.dot(basis, coef, precision=highest, preferred_element_type=jnp.float32)

    terms_one = project(lax.all_gather(block, "cols", axis=1, tiled=True))
    coef_one = lax.psum(terms_one, "rows")
    placed = lax.dynamic_update_slice_in_dim(
        jnp.zeros((local_rows, coef_one.shape[1]), jnp.float32), block, column_index * width, 1
    )
    first_whole = lax.psum(placed - expand(coef_one), "cols")
    terms_two = project(first_whole)
    first = lax.dynamic_slice_in_dim(first_whole, column_index * width, width, 1)
    coef_two = lax.psum(terms_two, "rows")
    second = first - lax.psum_scatter(expand(coef_two), "cols", scatter_dimension=1, tiled=True)
    blocks = width // BLK
    pieces = second.reshape(local_rows, blocks, BLK)
    gram = jnp.einsum("mbi,mbj->bij", pieces, pieces, precision=highest) * inverse
    gram = lax.psum(gram, "rows")
    lower_factor = jnp.linalg.cholesky(gram)
    solved = jax.vmap(solve_block)(lower_factor, jnp.transpose(pieces, (1, 2, 0)))
    ortho = jnp.transpose(solved, (2, 0, 1)).reshape(local_rows, width)
    return (ortho, jnp.transpose(lower_factor, (0, 2, 1)))


def solution(mesh):
    placed = (P("rows", "cols"), P("rows", "cols"))
    return jax.shard_map(
        body,
        mesh=mesh,
        in_specs=placed,
        out_specs=(P("rows", "cols"), P("cols", None, None)),
        check_vma=False,
    )
```

profile of v0, /device:TPU:0, one launch (start us, length us, event | category | flops | bytes accessed | tf_op | source)
XLA Modules:
  0.0 476.0 jit_solution(7517272405939530119)
XLA Ops:
  7.2 0.0 all-gather.2.cloned.1.call-start
  7.2 0.7 all-gather.2.cloned.1.call-update
  7.9 0.0 all-reduce.5.cloned.1.call-start
  7.9 27.2 %all-gather.2.cloned.1.call-done = f32[1024,512]{1,0:T(8,128)} async-done(((f32[1024,128]{1,0:T(8,128)}), f32[1024,512]{1,0:T(8,128)}) %all-gather.2.cloned.1.call-update) | async-done | bytes 2097168 | tf_op jit(solution)/shard_map/all_gather | solution.py:35
  35.1 10.2 %convolution_multiply_fusion = f32[1024,512]{1,0:T(8,128)} fusion(f32[1024,1024]{1,0:T(8,128)} %param.2, f32[1024,512]{1,0:T(8,128)} %all-gather.2.cloned.1.call-done), kind=kOutput, calls=%fused_computation.3 | convolution fusion | flops 6442975232 | bytes 8388608 | tf_op jit(solution)/shard_map/dot_general | solution.py:22
  45.3 0.0 copy-start.1
  45.3 0.0 all-reduce.5.cloned.1.call-update
  45.3 0.0 all-reduce.7.cloned.1.call-start
  45.4 1.0 copy-done.1
  46.3 0.2 copy.4
  46.5 0.2 broadcast_in_dim.7
  46.8 0.1 constant_dynamic-update-slice_fusion
  46.8 100.9 %all-reduce.5.cloned.1.call-done = f32[1024,512]{1,0:T(8,128)} async-done(((f32[1024,512]{1,0:T(8,128)}), f32[1024,512]{1,0:T(8,128)}) %all-reduce.5.cloned.1.call-update) | async-done | bytes 2097168 | tf_op jit(solution)/shard_map/psum | solution.py:36
  147.8 16.7 %bitcast_subtract_fusion = f32[1024,512]{0,1:T(8,128)} fusion(f32[1024,512]{0,1:T(8,128)S(1)} %constant_dynamic-update-slice_fusion, f32[1024,512]{1,0:T(8,128)} %all-reduce.5.cloned.1.call-done, f32[1024,1024]{1,0:T(8,128)} %param.2), kind=kOutput, calls=%fused_computation | convolution fusion | flops 6442975232 | bytes 10485760 | tf_op jit(solution)/shard_map/dot_general | solution.py:33
  164.5 0.0 all-reduce.7.cloned.1.call-update
  164.5 0.2 all-reduce.9.cloned.1.call-start
  164.7 50.6 %all-reduce.7.cloned.1.call-done = f32[1024,512]{0,1:T(8,128)} async-done(((f32[1024,512]{0,1:T(8,128)}), f32[1024,512]{0,1:T(8,128)}) %all-reduce.7.cloned.1.call-update) | async-done | bytes 2097168 | tf_op jit(solution)/shard_map/psum | solution.py:40
  215.3 10.2 %multiply_bitcast_fusion = f32[1024,512]{0,1:T(8,128)} fusion(f32[1024,512]{0,1:T(8,128)} %all-reduce.7.cloned.1.call-done, f32[1024,1024]{1,0:T(8,128)} %param.2), kind=kOutput, calls=%fused_computation.1 | convolution fusion | flops 6442975232 | bytes 8388608 | tf_op jit(solution)/shard_map/dot_general | solution.py:22
  225.6 0.0 all-reduce.9.cloned.1.call-update
  225.6 0.0 reduce-scatter.2.cloned.1.call-start
  225.6 102.5 %all-reduce.9.cloned.1.call-done = f32[1024,512]{0,1:T(8,128)} async-done(((f32[1024,512]{0,1:T(8,128)}), f32[1024,512]{0,1:T(8,128)}) %all-reduce.9.cloned.1.call-update) | async-done | bytes 2097168 | tf_op jit(solution)/shard_map/psum | solution.py:43
  328.1 10.3 %convolution_bitcast_fusion = f32[1024,512]{0,1:T(8,128)} fusion(f32[1024,512]{0,1:T(8,128)} %all-reduce.9.cloned.1.call-done, f32[1024,1024]{1,0:T(8,128)} %param.2), kind=kOutput, calls=%fused_computation.2 | convolution fusion | flops 6442450944 | bytes 8388608 | tf_op jit(solution)/shard_map/dot_general | solution.py:33
  338.4 0.0 copy-start
  338.4 0.0 reduce-scatter.2.cloned.1.call-update
  338.4 0.3 all-reduce.11.cloned.1.call-start
  338.7 30.3 %reduce-scatter.2.cloned.1.call-done = f32[1024,128]{0,1:T(8,128)} async-done(((f32[1024,512]{0,1:T(8,128)}), f32[1024,128]{0,1:T(8,128)}) %reduce-scatter.2.cloned.1.call-update) | async-done | bytes 524304 | tf_op jit(solution)/shard_map/reduce_scatter | solution.py:44
  369.0 0.0 copy-done
  369.0 0.0 copy-start.2
  369.0 2.5 fusion
  371.5 0.0 all-reduce.11.cloned.1.call-update
  371.5 70.6 %all-reduce.11.cloned.1.call-done = f32[1,128,128]{1,2,0:T(8,128)} async-done(((f32[1,128,128]{1,2,0:T(8,128)}), f32[1,128,128]{1,2,0:T(8,128)}) %all-reduce.11.cloned.1.call-update) | async-done | bytes 65552 | tf_op jit(solution)/shard_map/psum | solution.py:48
  442.2 0.9 copy.6
  443.1 0.9 fusion.3
  444.0 11.7 %custom-call.8 = f32[1,128,128]{2,1,0:T(8,128)S(1)} custom-call(f32[1,128,128]{2,1,0:T(8,128)S(1)} %fusion.3), custom_call_target="Cholesky" | custom-call | tf_op jit(solution)/shard_map/jit(cholesky)/cholesky | solution.py:49
  455.7 0.6 compare_reduce_fusion
  456.4 0.7 fusion.4
  457.0 9.8 %custom-call.9 = f32[1,1,128,128]{2,3,1,0:T(8,128)S(1)} custom-call(f32[1,1,128,128]{3,2,1,0:T(8,128)S(1)} %get-tuple-element.5), custom_call_target="InvertDiagBlocksLowerTriangular" | custom-call | tf_op jit(solution)/shard_map/vmap(jit(_solve_triangular))/triangular_solve | solution.py:10
  466.8 0.0 copy-done.2
  466.8 0.6 convolution_bitcast_fusion.1
  467.5 1.0 copy.7
  468.5 0.7 copy.8
  (1 shorter events, 0.0 us)
Async XLA Ops:
  7.2 27.9 %all-gather.2.cloned.1.call-start = ((), (), s32[]{:S(2)}) async-start(), calls=%async_computation.1 | async-start | bytes 2621440 | tf_op jit(solution)/shard_map/all_gather | solution.py:35
  7.9 139.9 %all-reduce.5.cloned.1.call-start = ((), (), s32[]{:S(2)}) async-start(), calls=%async_computation.2 | async-start | bytes 4194304 | tf_op jit(solution)/shard_map/psum | solution.py:36
  45.3 1.0 copy-start.1
  45.3 170.0 %all-reduce.7.cloned.1.call-start = ((), (), s32[]{:S(2)}) async-start(), calls=%async_computation.3 | async-start | bytes 4194304 | tf_op jit(solution)/shard_map/psum | solution.py:40
  164.5 163.6 %all-reduce.9.cloned.1.call-start = ((), (), s32[]{:S(2)}) async-start(), calls=%async_computation.4 | async-start | bytes 4194304 | tf_op jit(solution)/shard_map/psum | solution.py:43
  225.6 143.4 %reduce-scatter.2.cloned.1.call-start = ((), (), s32[]{:S(2)}) async-start(), calls=%async_computation.5 | async-start | bytes 2621440 | tf_op jit(solution)/shard_map/reduce_scatter | solution.py:44
  338.4 30.6 %copy-start = (f32[1024,512]{0,1:T(8,128)S(1)}, f32[1024,512]{0,1:T(8,128)}, u32[]{:S(2)}) copy-start(f32[1024,512]{0,1:T(8,128)} %all-reduce.7.cloned.1.call-done) | copy-start | bytes 6291460
  338.4 103.8 %all-reduce.11.cloned.1.call-start = ((), (), s32[]{:S(2)}) async-start(), calls=%async_computation.6 | async-start | bytes 131072 | tf_op jit(solution)/shard_map/psum | solution.py:48
  369.0 97.8 %copy-start.2 = (f32[1024,128]{0,1:T(8,128)S(1)}, f32[1024,128]{0,1:T(8,128)}, u32[]{:S(2)}) copy-start(f32[1024,128]{0,1:T(8,128)} %reduce-scatter.2.cloned.1.call-done) | copy-start | bytes 1572868
Sparse Core Ops, SparseCore 0:
  9.5 25.5 all-gather.1
  45.4 102.3 all-reduce.4
  164.6 50.6 all-reduce.6
  225.7 102.3 all-reduce.8
  338.5 30.4 reduce-scatter.1
  372.9 69.2 all-reduce.10
where the time goes:
time: 476 us
  waiting for transfers between devices  383 us (80%)
  matrix products  50.5 us (11%)
  other arithmetic  23.7 us (5%)
  between operations  14.2 us (3%)
    psum x1, waiting for transfers between devices, body(): coef_two = lax.psum(terms_two, 'rows')  102 us
    psum x1, waiting for transfers between devices, body(): coef_one = lax.psum(terms_one, 'rows')  101 us
    psum x1, waiting for transfers between devices, body(): gram = lax.psum(gram, 'rows')  70.6 us
    psum x1, waiting for transfers between devices, body(): first_whole = lax.psum(placed - expand(coef_one), 'cols')  50.6 us
    reduce_scatter x1, waiting for transfers between devices, body(): lax.psum_scatter(expand(coef_two), 'cols', scatter_dimension=1, tiled=True)  30.3 us
    all_gather x1, waiting for transfers between devices, body(): terms_one = project(lax.all_gather(block, 'cols', axis=1, tiled=True))  27.2 us
    dot_general x2, matrix products, expand(): jnp.dot(basis, coef, precision=highest, preferred_element_type=jnp.float32)  27 us
    dot_general x2, matrix products, project(): lax.dot_general(basis, piece, (((0,), (0,)), ((), ())), precision=highest...  20.4 us
  transfers between devices with their start and end apart: 6, of which 6 were waited for; matrix products, arithmetic and copies ran while one was open for 0% of the time, Pallas kernels for 0%

commit v1 on v0

--- a/solution.py
+++ b/solution.py
@@ -33,7 +33,9 @@
         return jnp.dot(basis, coef, precision=highest, preferred_element_type=jnp.float32)
 
     terms_one = project(lax.all_gather(block, "cols", axis=1, tiled=True))
-    coef_one = lax.psum(terms_one, "rows")
+    coef_one = terms_one
+    for hop in (1, 2, 4):
+        coef_one = coef_one + lax.ppermute(coef_one, "rows", [(dev, dev ^ hop) for dev in range(8)])
     placed = lax.dynamic_update_slice_in_dim(
         jnp.zeros((local_rows, coef_one.shape[1]), jnp.float32), block, column_index * width, 1
     )

time: 476 us -> 561 us (1.18)
  waiting for transfers between devices: 383 us -> 463 us
    ppermute x0 -> x3, waiting for transfers between devices: none -> 181 us  [body(): lax.ppermute(coef_one, 'rows', [(dev, dev ^ hop) for dev in range(8)])]
    psum x1 -> x0, waiting for transfers between devices: 101 us -> none  [body(): coef_one = lax.psum(terms_one, 'rows')]
  transfers between devices with their start and end apart: 6 -> 8, of which waited for: 6 -> 8; matrix products, arithmetic and copies ran while one was open for 0% -> 0% of each run, Pallas kernels for 0% -> 0%
where the time goes in v1:
time: 561 us
  waiting for transfers between devices  463 us (83%)
  matrix products  49.6 us (9%)
  other arithmetic  24.7 us (4%)
  between operations  13.9 us (2%)
  starting transfers between devices  6.16 us (1%)
    ppermute x3, waiting for transfers between devices, body(): lax.ppermute(coef_one, 'rows', [(dev, dev ^ hop) for dev in range(8)])  181 us
    psum x1, waiting for transfers between devices, body(): coef_two = lax.psum(terms_two, 'rows')  102 us
    psum x1, waiting for transfers between devices, body(): gram = lax.psum(gram, 'rows')  70.6 us
    psum x1, waiting for transfers between devices, body(): first_whole = lax.psum(placed - expand(coef_one), 'cols')  51.3 us
    reduce_scatter x1, waiting for transfers between devices, body(): lax.psum_scatter(expand(coef_two), 'cols', scatter_dimension=1, tiled=True)  30.3 us
    all_gather x1, waiting for transfers between devices, body(): terms_one = project(lax.all_gather(block, 'cols', axis=1, tiled=True))  27.2 us
    dot_general x2, matrix products, expand(): jnp.dot(basis, coef, precision=highest, preferred_element_type=jnp.float32)  27 us
    dot_general x2, matrix products, project(): lax.dot_general(basis, piece, (((0,), (0,)), ((), ())), precision=highest...  19.5 us
  transfers between devices with their start and end apart: 8, of which 8 were waited for; matrix products, arithmetic and copies ran while one was open for 0% of the time, Pallas kernels for 0%

profile of v1, /device:TPU:0, one launch (start us, length us, event | category | flops | bytes accessed | tf_op | source)
XLA Modules:
  0.0 560.9 jit_solution(2306049510241651862)
XLA Ops:
  7.2 0.0 all-gather.2.cloned.1.call-start
  7.2 0.7 all-gather.2.cloned.1.call-update
  7.9 0.0 all-reduce.4.cloned.1.call-start
  7.9 27.2 %all-gather.2.cloned.1.call-done = f32[1024,512]{1,0:T(8,128)} async-done(((f32[1024,128]{1,0:T(8,128)}), f32[1024,512]{1,0:T(8,128)}) %all-gather.2.cloned.1.call-update) | async-done | bytes 2097168 | tf_op jit(solution)/shard_map/all_gather | solution.py:35
  35.1 9.2 %convolution_multiply_fusion = f32[1024,512]{1,0:T(8,128)S(1)} fusion(f32[1024,1024]{1,0:T(8,128)} %param.2, f32[1024,512]{1,0:T(8,128)} %all-gather.2.cloned.1.call-done), kind=kOutput, calls=%fused_computation.5 | convolution fusion | flops 6442975232 | bytes 8388608 | tf_op jit(solution)/shard_map/dot_general | solution.py:22
  44.3 1.5 collective-permute-start
  45.9 46.3 %collective-permute-done = f32[1024,512]{1,0:T(8,128)S(1)} collective-permute-done((f32[1024,512]{1,0:T(8,128)S(1)}, f32[1024,512]{1,0:T(8,128)S(1)}, u32[]{:S(2)}, u32[]{:S(2)}) %collective-permute-start) | collective-permute-done | bytes 2097184 | tf_op jit(solution)/shard_map/ppermute | solution.py:38
  92.2 0.5 add.34
  92.7 0.0 copy-start.1
  92.7 1.6 collective-permute-start.1
  94.2 45.4 %collective-permute-done.1 = f32[1024,512]{1,0:T(8,128)S(1)} collective-permute-done((f32[1024,512]{1,0:T(8,128)S(1)}, f32[1024,512]{1,0:T(8,128)S(1)}, u32[]{:S(2)}, u32[]{:S(2)}) %collective-permute-start.1) | collective-permute-done | bytes 2097184 | tf_op jit(solution)/shard_map/ppermute | solution.py:38
  139.7 0.5 add.35
  140.1 2.5 collective-permute-start.2
  142.6 0.0 copy-done.1
  142.6 0.2 copy.4
  142.8 0.2 broadcast_in_dim.7
  143.1 0.1 constant_dynamic-update-slice_fusion
  143.1 89.1 %collective-permute-done.2 = f32[1024,512]{1,0:T(8,128)} collective-permute-done((f32[1024,512]{1,0:T(8,128)S(1)}, f32[1024,512]{1,0:T(8,128)}, u32[]{:S(2)}, u32[]{:S(2)}) %collective-permute-start.2) | collective-permute-done | bytes 2097184 | tf_op jit(solution)/shard_map/ppermute | solution.py:38
  232.2 16.7 %bitcast_subtract_fusion = f32[1024,512]{0,1:T(8,128)} fusion(f32[1024,512]{0,1:T(8,128)S(1)} %constant_dynamic-update-slice_fusion, f32[1024,1024]{1,0:T(8,128)} %param.2, f32[1024,512]{1,0:T(8,128)S(1)} %add.35, f32[1024,512]{1,0:T(8,128)} %collective-permute-done.2), kind=kOutput, calls=%fused_computation | convolution fusion | flops 6443499520 | bytes 12582912 | tf_op jit(solution)/shard_map/dot_general | solution.py:33
  248.9 0.0 all-reduce.4.cloned.1.call-update
  248.9 0.2 all-reduce.6.cloned.1.call-start
  249.2 51.3 %all-reduce.4.cloned.1.call-done = f32[1024,512]{0,1:T(8,128)} async-done(((f32[1024,512]{0,1:T(8,128)}), f32[1024,512]{0,1:T(8,128)}) %all-reduce.4.cloned.1.call-update) | async-done | bytes 2097168 | tf_op jit(solution)/shard_map/psum | solution.py:42
  300.4 10.3 %multiply_bitcast_fusion = f32[1024,512]{0,1:T(8,128)} fusion(f32[1024,512]{0,1:T(8,128)} %all-reduce.4.cloned.1.call-done, f32[1024,1024]{1,0:T(8,128)} %param.2), kind=kOutput, calls=%fused_computation.1 | convolution fusion | flops 6442975232 | bytes 8388608 | tf_op jit(solution)/shard_map/dot_general | solution.py:22
  310.7 0.0 all-reduce.6.cloned.1.call-update
  310.8 0.0 reduce-scatter.2.cloned.1.call-start
  310.8 102.5 %all-reduce.6.cloned.1.call-done = f32[1024,512]{0,1:T(8,128)} async-done(((f32[1024,512]{0,1:T(8,128)}), f32[1024,512]{0,1:T(8,128)}) %all-reduce.6.cloned.1.call-update) | async-done | bytes 2097168 | tf_op jit(solution)/shard_map/psum | solution.py:45
  413.3 10.3 %convolution_bitcast_fusion = f32[1024,512]{0,1:T(8,128)} fusion(f32[1024,512]{0,1:T(8,128)} %all-reduce.6.cloned.1.call-done, f32[1024,1024]{1,0:T(8,128)} %param.2), kind=kOutput, calls=%fused_computation.4 | convolution fusion | flops 6442450944 | bytes 8388608 | tf_op jit(solution)/shard_map/dot_general | solution.py:33
  423.6 0.0 copy-start
  423.6 0.0 reduce-scatter.2.cloned.1.call-update
  423.6 0.3 all-reduce.8.cloned.1.call-start
  423.9 30.3 %reduce-scatter.2.cloned.1.call-done = f32[1024,128]{0,1:T(8,128)} async-done(((f32[1024,512]{0,1:T(8,128)}), f32[1024,128]{0,1:T(8,128)}) %reduce-scatter.2.cloned.1.call-update) | async-done | bytes 524304 | tf_op jit(solution)/shard_map/reduce_scatter | solution.py:46
  454.2 0.0 copy-done
  454.2 0.0 copy-start.2
  454.2 2.5 fusion.4
  456.7 0.0 all-reduce.8.cloned.1.call-update
  456.7 70.6 %all-reduce.8.cloned.1.call-done = f32[1,128,128]{1,2,0:T(8,128)} async-done(((f32[1,128,128]{1,2,0:T(8,128)}), f32[1,128,128]{1,2,0:T(8,128)}) %all-reduce.8.cloned.1.call-update) | async-done | bytes 65552 | tf_op jit(solution)/shard_map/psum | solution.py:50
  527.3 0.9 copy.6
  528.3 0.9 fusion.7
  529.1 11.7 %custom-call.8 = f32[1,128,128]{2,1,0:T(8,128)S(1)} custom-call(f32[1,128,128]{2,1,0:T(8,128)S(1)} %fusion.7), custom_call_target="Cholesky" | custom-call | tf_op jit(solution)/shard_map/jit(cholesky)/cholesky | solution.py:51
  540.9 0.6 compare_reduce_fusion
  541.5 0.7 fusion.8
  542.2 0.7 copy.8
  542.9 9.8 %custom-call.9 = f32[1,1,128,128]{2,3,1,0:T(8,128)S(1)} custom-call(f32[1,1,128,128]{3,2,1,0:T(8,128)S(1)} %get-tuple-element.5), custom_call_target="InvertDiagBlocksLowerTriangular" | custom-call | tf_op jit(solution)/shard_map/vmap(jit(_solve_triangular))/triangular_solve | solution.py:10
  552.7 0.0 copy-done.2
  552.7 0.6 convolution_bitcast_fusion.1
  553.4 1.0 copy.7
  (1 shorter events, 0.0 us)
Async XLA Ops:
  7.2 27.9 %all-gather.2.cloned.1.call-start = ((), (), s32[]{:S(2)}) async-start(), calls=%async_computation.1 | async-start | bytes 2621440 | tf_op jit(solution)/shard_map/all_gather | solution.py:35
  7.9 292.5 %all-reduce.4.cloned.1.call-start = ((), (), s32[]{:S(2)}) async-start(), calls=%async_computation.2 | async-start | bytes 4194304 | tf_op jit(solution)/shard_map/psum | solution.py:42
  44.3 47.8 %collective-permute-start = (f32[1024,512]{1,0:T(8,128)S(1)}, f32[1024,512]{1,0:T(8,128)S(1)}, u32[]{:S(2)}, u32[]{:S(2)}) collective-permute-start(f32[1024,512]{1,0:T(8,128)S(1)} %convolution_multiply_fusion), channel_id=1, source_target_pairs={{0,4},{4,0},{8,12},{12,8},{16,20},{20,16},{24,28},{28,24},{1,5},{5... | collective-permute-start | bytes 6291464 | tf_op jit(solution)/shard_map/ppermute | solution.py:38
  92.7 50.0 %copy-start.1 = (f32[1024,128]{1,0:T(8,128)S(1)}, f32[1024,128]{1,0:T(8,128)}, u32[]{:S(2)}) copy-start(f32[1024,128]{1,0:T(8,128)} %param.3) | copy-start | bytes 1572868
  92.7 47.0 %collective-permute-start.1 = (f32[1024,512]{1,0:T(8,128)S(1)}, f32[1024,512]{1,0:T(8,128)S(1)}, u32[]{:S(2)}, u32[]{:S(2)}) collective-permute-start(f32[1024,512]{1,0:T(8,128)S(1)} %add.34), channel_id=1, source_target_pairs={{0,8},{4,12},{8,0},{12,4},{16,24},{20,28},{24,16},{28,20},{1,9},{5... | collective-permute-start | bytes 6291464 | tf_op jit(solution)/shard_map/ppermute | solution.py:38
  140.1 92.1 %collective-permute-start.2 = (f32[1024,512]{1,0:T(8,128)S(1)}, f32[1024,512]{1,0:T(8,128)}, u32[]{:S(2)}, u32[]{:S(2)}) collective-permute-start(f32[1024,512]{1,0:T(8,128)S(1)} %add.35), channel_id=1, source_target_pairs={{0,16},{4,20},{8,24},{12,28},{16,0},{20,4},{24,8},{28,12},{1,17},{... | collective-permute-start | bytes 6291464 | tf_op jit(solution)/shard_map/ppermute | solution.py:38
  248.9 164.3 %all-reduce.6.cloned.1.call-start = ((), (), s32[]{:S(2)}) async-start(), calls=%async_computation.3 | async-start | bytes 4194304 | tf_op jit(solution)/shard_map/psum | solution.py:45
  310.8 143.5 %reduce-scatter.2.cloned.1.call-start = ((), (), s32[]{:S(2)}) async-start(), calls=%async_computation.4 | async-start | bytes 2621440 | tf_op jit(solution)/shard_map/reduce_scatter | solution.py:46
  423.6 30.6 %copy-start = (f32[1024,512]{0,1:T(8,128)S(1)}, f32[1024,512]{0,1:T(8,128)}, u32[]{:S(2)}) copy-start(f32[1024,512]{0,1:T(8,128)} %all-reduce.4.cloned.1.call-done) | copy-start | bytes 6291460
  423.6 103.7 %all-reduce.8.cloned.1.call-start = ((), (), s32[]{:S(2)}) async-start(), calls=%async_computation.5 | async-start | bytes 131072 | tf_op jit(solution)/shard_map/psum | solution.py:50
  454.2 98.5 %copy-start.2 = (f32[1024,128]{0,1:T(8,128)S(1)}, f32[1024,128]{0,1:T(8,128)}, u32[]{:S(2)}) copy-start(f32[1024,128]{0,1:T(8,128)} %reduce-scatter.2.cloned.1.call-done) | copy-start | bytes 1572868
Sparse Core Ops, SparseCore 0:
  9.5 25.5 all-gather.1
  249.0 51.3 all-reduce.3
  310.9 102.3 all-reduce.5
  423.7 30.4 reduce-scatter.1
  458.0 69.2 all-reduce.7
